TPU v7x, 32 devices: a whole 2x2x4 slice. The times are simulated.
32 devices in a mesh: dp: 8 (over y, x, core), tensor: 4 (over z).
Axes of the slice: x: 2, y: 2, z: 4, core: 2. Of those that a mesh axis runs over, the one named last changes fastest.
Arguments:
- tokens: bfloat16 [32, 256, 1152], P(('dp', 'tensor')), may hold values from -6 to 6
- timesteps: int32 [32], P('dp'), may hold values from 0 to 999
- labels: int32 [32], P('dp'), may hold values from 0 to 999
- item_counts: int32 [8], P('dp'), may hold values from 1 to 4
- cotangent: bfloat16 [32, 256, 1152], P(('dp', 'tensor')), may hold values from -6 to 6
- project_weight: bfloat16 [1152, 3, 1152], P(None, None, 'tensor'), may hold values from -0.1875 to 0.1875
- query_gain: bfloat16 [72], replicated, may hold values from 0.099609375 to 1.8984375
- key_gain: bfloat16 [72], replicated, may hold values from 0.099609375 to 1.8984375
- output_weight: bfloat16 [1152, 1152], P('tensor'), may hold values from -0.5 to 0.5
- output_bias: bfloat16 [1152], replicated, may hold values from -3 to 3
- expand_weight: bfloat16 [1152, 2, 3072], P(None, None, 'tensor'), may hold values from -0.1875 to 0.1875
- down_weight: bfloat16 [3072, 1152], P('tensor'), may hold values from -0.15625 to 0.15625
- down_bias: bfloat16 [1152], replicated, may hold values from -3 to 3
- modulate_weight: bfloat16 [1152, 6, 1152], P(None, None, 'tensor'), may hold values from -0.1875 to 0.1875
- modulate_bias: bfloat16 [6, 1152], P(None, 'tensor'), may hold values from -3 to 3
- time_weight: bfloat16 [256, 1152], replicated, may hold values from -0.5 to 0.5
- time_bias: bfloat16 [1152], replicated, may hold values from -3 to 3
- embed_weight: bfloat16 [1152, 1152], replicated, may hold values from -0.25 to 0.25
- embed_bias: bfloat16 [1152], replicated, may hold values from -3 to 3
- class_table: bfloat16 [1000, 1152], replicated, may hold values from -6 to 6
Outputs:
- result: bfloat16 [32, 256, 1152], P(('dp', 'tensor'))
- tokens_grad: bfloat16 [32, 256, 1152], P(('dp', 'tensor'))
- project_grad: float32 [1152, 3, 1152], P('dp', None, 'tensor')
- query_gain_grad: float32 [72], replicated
- key_gain_grad: float32 [72], replicated
- output_weight_grad: float32 [1152, 1152], P('tensor', 'dp')
- output_bias_grad: float32 [1152], replicated
- expand_grad: float32 [1152, 2, 3072], P('dp', None, 'tensor')
- down_grad: float32 [3072, 1152], P('tensor', 'dp')
- down_bias_grad: float32 [1152], replicated
- modulate_grad: float32 [1152, 6, 1152], P('dp', None, 'tensor')
- modulate_bias_grad: float32 [6, 1152], replicated
- time_grad: float32 [256, 1152], P(None, 'dp')
- time_bias_grad: float32 [1152], P('dp')
- embed_grad: float32 [1152, 1152], P('dp')
- embed_bias_grad: float32 [1152], P('dp')
- class_grad: float32 [1000, 1152], P(None, 'dp')
Inputs may be any that keep to these rules, and one draw needn't show every extreme that they name: `item_counts`: entry i counts the real items among the 4 items of index i of dp; they are its first ones.
All inputs are finite; a program needn't handle non-finite values.
Results may differ from a plain program's by a relative error of at most 0.03.
Values may be sent and summed in bfloat16 or wider, within the bound.
A program may use at most 256 MiB of HBM per device.

v0:
```python
import math
import jax
import jax.numpy as jnp
from jax import lax
from jax.sharding import PartitionSpec as P

HD = 72
FREQ = 256
GRID = 16
EPS = 1e-06


def layer_norm(value):
    center = value - jnp.mean(value, axis=-1, keepdims=True)
    inverse = lax.rsqrt(jnp.mean(center * center, axis=-1, keepdims=True) + EPS)
    return (center * inverse, inverse)


def layer_norm_back(normed, inverse, grad):
    return inverse * (
        grad
        - jnp.mean(grad, axis=-1, keepdims=True)
        - normed * jnp.mean(grad * normed, axis=-1, keepdims=True)
    )


def silu_slope(value):
    sigma = jax.nn.sigmoid(value)
    return sigma * (1.0 + value * (1.0 - sigma))


def rotate(value, positions):
    quarter = HD // 4
    rates = 10000.0 ** (-jnp.arange(quarter, dtype=jnp.float32) / quarter)
    places = ((positions // GRID).astype(jnp.float32), (positions % GRID).astype(jnp.float32))
    pieces = []
    for which_half in range(2):
        half_value = value[..., which_half * 2 * quarter : (which_half + 1) * 2 * quarter]
        angle = places[which_half][:, None] * rates[None, :]
        cosine = jnp.cos(angle)[None, :, None, :]
        sine = jnp.sin(angle)[None, :, None, :]
        first = half_value[..., :quarter]
        second = half_value[..., quarter:]
        pieces.append(first * cosine - second * sine)
        pieces.append(second * cosine + first * sine)
    return jnp.concatenate(pieces, axis=-1)


def head_prepare(raw, gain, positions):
    scaled = raw * lax.rsqrt(jnp.mean(raw * raw, axis=-1, keepdims=True) + EPS) * gain
    return rotate(scaled, positions)


def time_features(steps_in):
    half = FREQ // 2
    rates = jnp.exp(-math.log(10000.0) * jnp.arange(half, dtype=jnp.float32) / half)
    angle = steps_in.astype(jnp.float32)[:, None] * rates[None, :]
    return jnp.concatenate([jnp.cos(angle), jnp.sin(angle)], axis=-1)


def shards(
    tokens,
    timesteps,
    labels,
    item_counts,
    cotangent,
    project_weight,
    query_gain,
    key_gain,
    output_weight,
    output_bias,
    expand_weight,
    down_weight,
    down_bias,
    modulate_weight,
    modulate_bias,
    time_weight,
    time_bias,
    embed_weight,
    embed_bias,
    class_table,
):
    local_items, length, width = tokens.shape
    items = timesteps.shape[0]
    slab = modulate_weight.shape[2]
    heads_here = project_weight.shape[2] // HD
    scale = HD ** (-0.5)
    lane = lax.axis_index("tensor")
    first_item = lane * local_items
    live = (first_item + jnp.arange(local_items) < item_counts[0]).astype(jnp.float32)[
        :, None, None
    ]
    index = lax.axis_index("dp")
    tags = lax.all_gather(jnp.stack([timesteps, labels]), "dp", axis=1, tiled=True)
    time_feat = time_features(tags[0]).astype(jnp.bfloat16)
    pre_hidden = jnp.dot(
        time_feat, time_weight, preferred_element_type=jnp.float32
    ) + time_bias.astype(jnp.float32)
    time_hidden = jax.nn.silu(pre_hidden).astype(jnp.bfloat16)
    condition = (
        jnp.dot(time_hidden, embed_weight, preferred_element_type=jnp.float32)
        + embed_bias.astype(jnp.float32)
        + jnp.take(class_table, tags[1], axis=0).astype(jnp.float32)
    )
    cond_act = jax.nn.silu(condition).astype(jnp.bfloat16)
    cond_act_here = lax.dynamic_slice_in_dim(cond_act, index * items, items, 0)
    condition_here = lax.dynamic_slice_in_dim(condition, index * items, items, 0)
    modulation_part = (
        jnp.einsum(
            "bd,dke->bke", cond_act_here, modulate_weight, preferred_element_type=jnp.float32
        )
        + modulate_bias.astype(jnp.float32)
    ).astype(jnp.bfloat16)
    modulation_local = lax.all_to_all(
        modulation_part, "tensor", split_axis=0, concat_axis=2, tiled=True
    ).astype(jnp.float32)
    local_parts = [modulation_local[:, which][:, None, :] for which in range(6)]
    attend_shift, attend_scale, attend_gate, feed_shift, feed_scale, feed_gate = local_parts
    positions = jnp.arange(length)
    token_local = tokens.astype(jnp.float32)
    normed_local, inverse_local = layer_norm(token_local)
    mod_in = lax.all_gather(
        (normed_local * (1.0 + attend_scale) + attend_shift).astype(jnp.bfloat16),
        "tensor",
        axis=0,
        tiled=True,
    )
    projected = jnp.einsum(
        "bld,dke->blke", mod_in, project_weight, preferred_element_type=jnp.float32
    )
    split = projected.reshape(items, length, 3, heads_here, HD)
    query_gain_f = query_gain.astype(jnp.float32)
    key_gain_f = key_gain.astype(jnp.float32)
    queries = head_prepare(split[:, :, 0], query_gain_f, positions).astype(jnp.bfloat16)
    keys = head_prepare(split[:, :, 1], key_gain_f, positions).astype(jnp.bfloat16)
    values = split[:, :, 2].astype(jnp.bfloat16)
    scores = (
        jnp.einsum("bqhd,bkhd->bhqk", queries, keys, preferred_element_type=jnp.float32) * scale
    )
    top = jnp.max(scores, axis=-1, keepdims=True)
    logsum = top + jnp.log(jnp.sum(jnp.exp(scores - top), axis=-1, keepdims=True))
    probs = jnp.exp(scores - logsum).astype(jnp.bfloat16)
    mixed = jnp.einsum("bhqk,bkhd->bqhd", probs, values, preferred_element_type=jnp.float32)
    mixed = mixed.reshape(items, length, heads_here * HD).astype(jnp.bfloat16)
    piece = mixed
    attend_branch = lax.psum_scatter(
        jnp.einsum("blh,hd->bld", piece, output_weight, preferred_element_type=jnp.float32).astype(
            jnp.bfloat16
        ),
        "tensor",
        scatter_dimension=0,
        tiled=True,
    ).astype(jnp.float32) + output_bias.astype(jnp.float32)
    residual = token_local + attend_gate * attend_branch
    normed_two, inverse_two = layer_norm(residual)
    mod_two = (normed_two * (1.0 + feed_scale) + feed_shift).astype(jnp.bfloat16)
    mod_two_all = lax.all_gather(mod_two, "tensor", axis=0, tiled=True)
    gate_up = jnp.einsum(
        "bld,dkf->blkf", mod_two_all, expand_weight, preferred_element_type=jnp.float32
    )
    gate = gate_up[:, :, 0]
    upper = gate_up[:, :, 1]
    hidden = (jax.nn.silu(gate) * upper).astype(jnp.bfloat16)
    piece = hidden
    feed_branch = lax.psum_scatter(
        jnp.einsum("blf,fd->bld", piece, down_weight, preferred_element_type=jnp.float32).astype(
            jnp.bfloat16
        ),
        "tensor",
        scatter_dimension=0,
        tiled=True,
    ).astype(jnp.float32) + down_bias.astype(jnp.float32)
    result = (live * (residual + feed_gate * feed_branch)).astype(jnp.bfloat16)
    out_grad = cotangent.astype(jnp.float32) * live
    branch_grad = (out_grad * feed_gate).astype(jnp.bfloat16)
    down_bias_part = jnp.sum(branch_grad.astype(jnp.float32), axis=(0, 1))
    piece = lax.all_gather(branch_grad, "tensor", axis=0, tiled=True)
    weight_total = jnp.einsum("blf,bld->fd", hidden, piece, preferred_element_type=jnp.float32)
    rows_grad = jnp.einsum("bld,fd->blf", piece, down_weight, preferred_element_type=jnp.float32)
    hidden_total = rows_grad
    down_grad = weight_total
    gate_up_grad = jnp.stack(
        [hidden_total * upper * silu_slope(gate), hidden_total * jax.nn.silu(gate)], axis=2
    ).astype(jnp.bfloat16)
    expand_grad = jnp.einsum(
        "bld,blkf->dkf", mod_two_all, gate_up_grad, preferred_element_type=jnp.float32
    )
    piece = gate_up_grad
    mod_two_grad = lax.psum_scatter(
        jnp.einsum(
            "blkf,dkf->bld", piece, expand_weight, preferred_element_type=jnp.float32
        ).astype(jnp.bfloat16),
        "tensor",
        scatter_dimension=0,
        tiled=True,
    ).astype(jnp.float32)
    residual_grad = out_grad + layer_norm_back(
        normed_two, inverse_two, mod_two_grad * (1.0 + feed_scale)
    )
    attend_grad = (residual_grad * attend_gate).astype(jnp.bfloat16)
    output_bias_part = jnp.sum(attend_grad.astype(jnp.float32), axis=(0, 1))
    piece = lax.all_gather(attend_grad, "tensor", axis=0, tiled=True)
    weight_total = jnp.einsum("blh,bld->hd", mixed, piece, preferred_element_type=jnp.float32)
    rows_grad = jnp.einsum("bld,hd->blh", piece, output_weight, preferred_element_type=jnp.float32)
    output_weight_grad = weight_total
    mixed_grad = rows_grad
    mixed_grad = mixed_grad.reshape(items, length, heads_here, HD).astype(jnp.bfloat16)
    again = jnp.einsum("bqhd,bkhd->bhqk", queries, keys, preferred_element_type=jnp.float32) * scale
    prob_float = jnp.exp(again - logsum)
    prob_low = prob_float.astype(jnp.bfloat16)
    prob_grad = jnp.einsum(
        "bqhd,bkhd->bhqk", mixed_grad, values, preferred_element_type=jnp.float32
    )
    score_grad = (
        prob_float * (prob_grad - jnp.sum(prob_float * prob_grad, axis=-1, keepdims=True))
    ).astype(jnp.bfloat16)
    query_grad = (
        jnp.einsum("bhqk,bkhd->bqhd", score_grad, keys, preferred_element_type=jnp.float32) * scale
    )
    key_grad = (
        jnp.einsum("bhqk,bqhd->bkhd", score_grad, queries, preferred_element_type=jnp.float32)
        * scale
    )
    value_grad = jnp.einsum(
        "bhqk,bqhd->bkhd", prob_low, mixed_grad, preferred_element_type=jnp.float32
    )

    def prepare_here(raw, gain):
        return head_prepare(raw, gain, positions)

    _, query_back = jax.vjp(prepare_here, split[:, :, 0], query_gain_f)
    raw_query_grad, query_gain_part = query_back(query_grad)
    _, key_back = jax.vjp(prepare_here, split[:, :, 1], key_gain_f)
    raw_key_grad, key_gain_part = key_back(key_grad)
    projected_grad = jnp.stack([raw_query_grad, raw_key_grad, value_grad], axis=2)
    projected_grad = projected_grad.reshape(items, length, 3, heads_here * HD).astype(jnp.bfloat16)
    project_grad = jnp.einsum(
        "bld,blke->dke", mod_in, projected_grad, preferred_element_type=jnp.float32
    )
    piece = projected_grad
    mod_in_grad = lax.psum_scatter(
        jnp.einsum(
            "blke,dke->bld", piece, project_weight, preferred_element_type=jnp.float32
        ).astype(jnp.bfloat16),
        "tensor",
        scatter_dimension=0,
        tiled=True,
    ).astype(jnp.float32)
    tokens_grad = (
        residual_grad
        + layer_norm_back(normed_local, inverse_local, mod_in_grad * (1.0 + attend_scale))
    ).astype(jnp.bfloat16)
    modulation_grad_part = jnp.stack(
        [
            jnp.sum(mod_in_grad, axis=1),
            jnp.sum(mod_in_grad * normed_local, axis=1),
            jnp.sum(residual_grad * attend_branch, axis=1),
            jnp.sum(mod_two_grad, axis=1),
            jnp.sum(mod_two_grad * normed_two, axis=1),
            jnp.sum(out_grad * feed_branch, axis=1),
        ],
        axis=1,
    )
    modulation_grad = lax.all_to_all(
        modulation_grad_part, "tensor", split_axis=2, concat_axis=0, tiled=True
    ).astype(jnp.bfloat16)
    modulate_bias_part = jnp.sum(modulation_grad.astype(jnp.float32), axis=0)
    cond_part = jnp.einsum(
        "bke,dke->bd", modulation_grad, modulate_weight, preferred_element_type=jnp.float32
    )
    cond_total = lax.psum(cond_part, "tensor")
    cond_grad_here = (cond_total * silu_slope(condition_here)).astype(jnp.bfloat16)
    packed = jnp.concatenate([cond_grad_here, modulation_grad.reshape(items, 6 * slab)], axis=1)
    packed = lax.all_gather(packed, "dp", axis=0, tiled=True)
    cond_grad = packed[:, :width]
    modulation_grad_all = packed[:, width:].reshape(-1, 6, slab)
    share = width // lax.axis_size("dp")

    def mine(value, axis):
        return lax.dynamic_slice_in_dim(value, index * share, share, axis)

    one_hot = (tags[1][:, None] == jnp.arange(class_table.shape[0])[None, :]).astype(jnp.bfloat16)
    cond_grad_mine = mine(cond_grad, 1)
    class_grad = jnp.einsum(
        "bc,bd->cd", one_hot, cond_grad_mine, preferred_element_type=jnp.float32
    )
    pre_grad = (
        jnp.einsum(
            "be,de->bd", cond_grad, mine(embed_weight, 0), preferred_element_type=jnp.float32
        )
        * silu_slope(mine(pre_hidden, 1))
    ).astype(jnp.bfloat16)
    modulate_grad = jnp.einsum(
        "bd,bke->dke", mine(cond_act, 1), modulation_grad_all, preferred_element_type=jnp.float32
    )
    embed_grad = jnp.einsum(
        "bd,be->de", mine(time_hidden, 1), cond_grad, preferred_element_type=jnp.float32
    )
    embed_bias_grad = jnp.sum(cond_grad_mine.astype(jnp.float32), axis=0)
    time_grad = jnp.einsum("bf,bd->fd", time_feat, pre_grad, preferred_element_type=jnp.float32)
    time_bias_grad = jnp.sum(pre_grad.astype(jnp.float32), axis=0)
    bias_wide = lax.dynamic_update_slice_in_dim(
        jnp.zeros((6, width), jnp.float32), modulate_bias_part, lane * slab, 1
    )
    small = jnp.concatenate(
        [output_bias_part, down_bias_part, bias_wide.reshape(-1), query_gain_part, key_gain_part]
    )
    small = lax.psum(small, ("dp", "tensor"))
    output_bias_grad = small[:width]
    down_bias_grad = small[width : 2 * width]
    modulate_bias_grad = small[2 * width : 8 * width].reshape(6, width)
    query_gain_grad = small[8 * width : 8 * width + HD]
    key_gain_grad = small[8 * width + HD :]

    def scatter(value, axis):
        value = value.astype(jnp.bfloat16)
        return lax.psum_scatter(value, "dp", scatter_dimension=axis, tiled=True).astype(jnp.float32)

    project_grad = scatter(project_grad, 0)
    output_weight_grad = scatter(output_weight_grad, 1)
    expand_grad = scatter(expand_grad, 0)
    down_grad = scatter(down_grad, 1)
    return (
        result,
        tokens_grad,
        project_grad,
        query_gain_grad,
        key_gain_grad,
        output_weight_grad,
        output_bias_grad,
        expand_grad,
        down_grad,
        down_bias_grad,
        modulate_grad,
        modulate_bias_grad,
        time_grad,
        time_bias_grad,
        embed_grad,
        embed_bias_grad,
        class_grad,
    )


def solution(mesh):
    return jax.shard_map(
        shards,
        mesh=mesh,
        in_specs=(
            P(("dp", "tensor"), None, None),
            P("dp"),
            P("dp"),
            P("dp"),
            P(("dp", "tensor"), None, None),
            P(None, None, "tensor"),
            P(),
            P(),
            P("tensor", None),
            P(),
            P(None, None, "tensor"),
            P("tensor", None),
            P(),
            P(None, None, "tensor"),
            P(None, "tensor"),
            P(),
            P(),
            P(),
            P(),
            P(),
        ),
        out_specs=(
            P(("dp", "tensor"), None, None),
            P(("dp", "tensor"), None, None),
            P("dp", None, "tensor"),
            P(),
            P(),
            P("tensor", "dp"),
            P(),
            P("dp", None, "tensor"),
            P("tensor", "dp"),
            P(),
            P("dp", None, "tensor"),
            P(),
            P(None, "dp"),
            P("dp"),
            P("dp", None),
            P("dp"),
            P(None, "dp"),
        ),
        check_vma=False,
    )
```

profile of v0, /device:TPU:0, one launch (start us, length us, event | category | flops | bytes accessed | tf_op | source)
XLA Modules:
  0.0 764.2 jit_solution(1192706459011180409)
XLA Ops:
  8.1 10.4 %all-gather = s32[8,4,2]{1,2,0:T(2,128)S(1)} all-gather(s32[1,4,2]{1,2,0:T(2,128)S(1)} %add_bitcast_fusion), channel_id=1, replica_groups=mesh['dp'=8,'tensor'=4] {'dp'}, dimensions={0}, use_global_device_ids=true | all-gather | bytes 288 | tf_op jit(solution)/shard_map/all_gather | solution.py:94
  21.4 2.6 gather_fusion
  24.0 2.1 multiply_convert_fusion.8
  26.2 1.2 multiply_convert_fusion.7
  27.4 1.3 fusion.49
  29.4 4.9 all-to-all-start
  34.8 5.1 all-to-all-done
  42.8 47.1 %all-gather.7.cloned.1.call-done = bf16[4,256,1152]{2,1,0:T(8,128)(2,1)} async-done(((bf16[1,256,1152]{2,1,0:T(8,128)(2,1)}), bf16[4,256,1152]{2,1,0:T(8,128)(2,1)}) %all-gather.7.cloned.1.call-update) | async-done | bytes 2359312 | tf_op jit(solution)/shard_map/all_gather | solution.py:122
  90.0 4.7 fusion.10
  98.6 1.2 multiply_reduce_fusion.1
  100.6 1.3 copy-done.1
  103.5 2.9 convolution_convert_fusion.1
  106.6 1.3 convert_element_type.316
  107.8 45.3 %reduce-scatter.9.cloned.1.call-done = bf16[1,256,1152]{2,1,0:T(8,128)(2,1)} async-done(((bf16[4,256,1152]{2,1,0:T(8,128)(2,1)}), bf16[1,256,1152]{2,1,0:T(8,128)(2,1)}) %reduce-scatter.9.cloned.1.call-update) | async-done | bytes 589840 | tf_op jit(solution)/shard_map/reduce_scatter | solution.py:146
  153.1 1.4 fusion.103
  155.6 1.2 add_convert_fusion
  157.6 2.7 convert_reduce_fusion.3
  160.6 45.8 %all-gather.9.cloned.1.call-done = bf16[4,256,1152]{2,1,0:T(8,128)(2,1)} async-done(((bf16[1,256,1152]{2,1,0:T(8,128)(2,1)}), bf16[4,256,1152]{2,1,0:T(8,128)(2,1)}) %all-gather.9.cloned.1.call-update) | async-done | bytes 2359312 | tf_op jit(solution)/shard_map/all_gather | solution.py:157
  206.4 9.6 %fusion.1 = f32[4,256,2,768]{3,1,2,0:T(8,128)} fusion(bf16[1152,2,768]{2,1,0:T(2,128)(2,1)} %param.30, bf16[4,256,1152]{2,1,0:T(8,128)(2,1)} %all-gather.9.cloned.1.call-done), kind=kOutput, calls=%fused_computation.14 | convolution fusion | flops 3623878656 | bytes 12189696 | tf_op jit(solution)/shard_map/bld,dkf->blkf/dot_general | solution.py:158
  216.0 41.2 %all-gather.11.cloned.1.call-done = bf16[4,256,1152]{2,1,0:T(8,128)(2,1)} async-done(((bf16[1,256,1152]{2,1,0:T(8,128)(2,1)}), bf16[4,256,1152]{2,1,0:T(8,128)(2,1)}) %all-gather.11.cloned.1.call-update) | async-done | bytes 2359312 | tf_op jit(solution)/shard_map/all_gather | solution.py:177
  257.2 8.4 %fusion.26 = (bf16[4,256,1,768]{3,1,0,2:T(8,128)(2,1)S(1)}, bf16[4,256,1,768]{3,1,0,2:T(8,128)(2,1)S(1)}, bf16[4,256,768]{2,1,0:T(8,128)(2,1)}) fusion(f32[4,256,2,768]{3,1,2,0:T(8,128)} %fusion.1, bf16[4,256,1152]{2,1,0:T(8,128)(2,1)} %all-gather.11.cloned.1.call-done, bf16[768,1152]{1,0:T(8,128)(2,1)} %param.31), kind=kOutput, calls=%fused_computation.62 | convolution fusion | flops 1823735808 | bytes 15138816 | tf_op jit(solution)/shard_map/bld,fd->blf/dot_general | solution.py:179
  265.6 1.2 copy-done.81
  267.2 5.6 bitcast_convert_fusion.3
  272.8 5.6 convolution_convert_fusion
  278.5 1.3 convert_element_type.321
  279.8 39.6 %reduce-scatter.13.cloned.1.call-done = bf16[1,256,1152]{2,1,0:T(8,128)(2,1)} async-done(((bf16[4,256,1152]{2,1,0:T(8,128)(2,1)}), bf16[1,256,1152]{2,1,0:T(8,128)(2,1)}) %reduce-scatter.13.cloned.1.call-update) | async-done | bytes 589840 | tf_op jit(solution)/shard_map/reduce_scatter | solution.py:189
  319.4 2.6 fusion.45
  323.2 45.5 %reduce-scatter.11.cloned.1.call-done = bf16[1,256,1152]{2,1,0:T(8,128)(2,1)} async-done(((bf16[4,256,1152]{2,1,0:T(8,128)(2,1)}), bf16[1,256,1152]{2,1,0:T(8,128)(2,1)}) %reduce-scatter.11.cloned.1.call-update) | async-done | bytes 589840 | tf_op jit(solution)/shard_map/reduce_scatter | solution.py:165
  368.7 4.1 multiply_reduce_fusion.5
  373.9 1.5 convert_reduce_fusion.4
  375.4 11.2 %reduce-scatter.23.cloned.1.call-start = ((), (), s32[]{:S(2)}) async-start(), calls=%async_computation.21 | async-start | bytes 1990656 | tf_op jit(solution)/shard_map/reduce_scatter | solution.py:317
  386.6 5.4 fusion.4
  392.1 8.2 %bitcast_convert_fusion = bf16[1152,2,768]{2,0,1:T(8,128)(2,1)} fusion(bf16[4,256,1152]{2,1,0:T(8,128)(2,1)} %all-gather.9.cloned.1.call-done, bf16[4,256,1,768]{3,1,0,2:T(8,128)(2,1)} %copy-done.82, bf16[4,256,1,768]{3,1,0,2:T(8,128)(2,1)} %copy-done.81), kind=kOutput, calls=%fused_computation.1 | convolution fusion | flops 3631939584 | bytes 9043968 | tf_op jit(solution)/shard_map/bld,blkf->dkf/dot_general | solution.py:185
  400.4 24.6 %all-gather.13.cloned.1.call-done = bf16[4,256,1152]{2,1,0:T(8,128)(2,1)} async-done(((bf16[1,256,1152]{2,1,0:T(8,128)(2,1)}), bf16[4,256,1152]{2,1,0:T(8,128)(2,1)}) %all-gather.13.cloned.1.call-update) | async-done | bytes 2359312 | tf_op jit(solution)/shard_map/all_gather | solution.py:202
  424.9 2.9 convolution_convert_fusion.3
  428.0 2.4 multiply_reduce_fusion
  438.8 1.2 fusion.47
  440.9 2.4 fusion.6
  443.3 2.0 fusion.46
  445.4 3.5 convolution_convert_fusion.2
  449.8 5.3 bitcast_convert_fusion.1
  455.4 6.5 bitcast_convert_fusion.2
  461.9 4.4 reduce-scatter.23.cloned.1.call-done
  466.3 1.7 convert_element_type.348
  468.1 49.6 %reduce-scatter.21.cloned.1.call-done = bf16[144,2,768]{2,0,1:T(8,128)(2,1)} async-done(((bf16[1152,2,768]{2,0,1:T(8,128)(2,1)}), bf16[144,2,768]{2,0,1:T(8,128)(2,1)}) %reduce-scatter.21.cloned.1.call-update) | async-done | bytes 442384 | tf_op jit(solution)/shard_map/reduce_scatter | solution.py:317
  517.7 2.3 copy.157
  520.0 35.5 %reduce-scatter.19.cloned.1.call-done = bf16[288,144]{0,1:T(8,128)(2,1)} async-done(((bf16[288,1152]{0,1:T(8,128)(2,1)}), bf16[288,144]{0,1:T(8,128)(2,1)}) %reduce-scatter.19.cloned.1.call-update) | async-done | bytes 82960 | tf_op jit(solution)/shard_map/reduce_scatter | solution.py:317
  555.4 1.6 convert_element_type.344
  557.0 44.9 %reduce-scatter.17.cloned.1.call-done = bf16[144,3,288]{2,0,1:T(8,128)(2,1)} async-done(((bf16[1152,3,288]{2,0,1:T(8,128)(2,1)}), bf16[144,3,288]{2,0,1:T(8,128)(2,1)}) %reduce-scatter.17.cloned.1.call-update) | async-done | bytes 248848 | tf_op jit(solution)/shard_map/reduce_scatter | solution.py:317
  602.0 1.9 convert_element_type.335
  603.8 48.0 %reduce-scatter.15.cloned.1.call-done = bf16[1,256,1152]{2,1,0:T(8,128)(2,1)} async-done(((bf16[4,256,1152]{2,1,0:T(8,128)(2,1)}), bf16[1,256,1152]{2,1,0:T(8,128)(2,1)}) %reduce-scatter.15.cloned.1.call-update) | async-done | bytes 589840 | tf_op jit(solution)/shard_map/reduce_scatter | solution.py:241
  651.9 1.7 fusion.48
  654.7 1.3 copy.150
  656.5 7.7 %reduce.26 = bf16[1152,6]{1,0:T(8,128)(2,1)S(1)} reduce(bf16[1152,1,6]{2,1,0:T(2,128)(2,1)} %bitcast.210, bf16[]{:T(256)} %broadcast.432), dimensions={1}, to_apply=%bitcast.178.reduce_sub_computation | reduce | bytes 27650
  665.2 3.3 all-to-all-start.1
  668.5 2.8 fusion.38
  671.2 2.8 all-to-all-done.1
  675.8 39.6 %psum.14 = f32[9360]{0:T(1024)S(1)} all-reduce(f32[9360]{0:T(1024)S(1)} %concatenate.23), channel_id=1, replica_groups=mesh['dp'=8,'tensor'=4] {'dp','tensor'}, use_global_device_ids=true, to_apply=%region_31.32 | all-reduce | flops 9360 | bytes 74880 | tf_op jit(solution)/shard_map/psum | solution.py:308
  716.6 2.8 convolution_bitcast_fusion.2
  719.4 17.1 %psum.15 = f32[4,1152]{1,0:T(4,128)S(1)} all-reduce(f32[4,1152]{1,0:T(4,128)S(1)} %convolution_bitcast_fusion.2), channel_id=1, replica_groups=mesh['dp'=8,'tensor'=4] {'tensor'}, use_global_device_ids=true, to_apply=%region_35.36 | all-reduce | flops 4608 | bytes 36864 | tf_op jit(solution)/shard_map/psum | solution.py:271
  737.5 10.0 %all-gather.1 = bf16[8,4,2880]{2,1,0:T(4,128)(2,1)S(1)} all-gather(bf16[1,4,2880]{2,1,0:T(4,128)(2,1)S(1)} %maximum_bitcast_fusion), channel_id=1, replica_groups=mesh['dp'=8,'tensor'=4] {'dp'}, dimensions={0}, use_global_device_ids=true | all-gather | bytes 207360 | tf_op jit(solution)/shard_map/all_gather | solution.py:274
  748.3 1.9 fusion.68
  750.2 1.6 convert_reduce_fusion.7
  754.7 2.2 fusion.60
  (277 shorter events, 38.6 us)
Async XLA Ops:
  7.2 19.0 %copy-start = (bf16[1152,1152]{1,0:T(8,128)(2,1)S(1)}, bf16[1152,1152]{1,0:T(8,128)(2,1)}, u32[]{:S(2)}) copy-start(bf16[1152,1152]{1,0:T(8,128)(2,1)} %param.37) | copy-start | bytes 7962628
  21.4 6.0 copy-start.54
  21.4 6.0 copy-start.56
  24.0 3.4 copy-start.8
  27.4 6.9 copy-start.3
  29.4 10.5 %all-to-all-start = ((bf16[4,6,288]{2,1,0:T(8,128)(2,1)}), bf16[4,6,288]{2,1,0:T(8,128)(2,1)S(1)}, u32[]{:S(2)}, u32[]{:S(2)}) async-start(bf16[4,6,288]{2,1,0:T(8,128)(2,1)} %copy.133), calls=%async_computation | async-start | bytes 49152 | tf_op jit(solution)/shard_map/all_to_all | solution.py:114
  34.3 55.7 %all-gather.7.cloned.1.call-start = ((), (), s32[]{:S(2)}) async-start(), calls=%async_computation.10 | async-start | bytes 2949120 | tf_op jit(solution)/shard_map/all_gather | solution.py:122
  34.4 8.0 %copy-start.58 = (f32[256]{0:T(256)}, f32[256]{0:T(256)S(1)}, u32[]{:S(2)}) copy-start(f32[256]{0:T(256)S(1)} %broadcast_multiply_fusion.5) | copy-start | bytes 3076
  34.8 7.7 %copy-start.79 = (bf16[72]{0:T(256)(128)(2,1)S(1)}, bf16[72]{0:T(256)(128)(2,1)}, u32[]{:S(2)}) copy-start(bf16[72]{0:T(256)(128)(2,1)} %param.26) | copy-start | bytes 436
  34.8 7.7 %copy-start.80 = (bf16[72]{0:T(256)(128)(2,1)S(1)}, bf16[72]{0:T(256)(128)(2,1)}, u32[]{:S(2)}) copy-start(bf16[72]{0:T(256)(128)(2,1)} %param.27) | copy-start | bytes 436
  34.8 59.9 %copy-start.61 = (f32[256]{0:T(256)}, f32[256]{0:T(256)S(1)}, u32[]{:S(2)}) copy-start(f32[256]{0:T(256)S(1)} %add_rsqrt_fusion.1) | copy-start | bytes 3076
  42.4 110.7 %reduce-scatter.9.cloned.1.call-start = ((), (), s32[]{:S(2)}) async-start(), calls=%async_computation.11 | async-start | bytes 2949120 | tf_op jit(solution)/shard_map/reduce_scatter | solution.py:146
  42.5 52.8 %copy-start.68 = (f32[72]{0:T(128)}, f32[72]{0:T(128)S(1)}, u32[]{:S(2)}) copy-start(f32[72]{0:T(128)S(1)} %convert_element_type.306) | copy-start | bytes 868
  42.5 53.9 %copy-start.70 = (f32[72]{0:T(128)}, f32[72]{0:T(128)S(1)}, u32[]{:S(2)}) copy-start(f32[72]{0:T(128)S(1)} %convert_element_type.309) | copy-start | bytes 868
  94.7 5.9 copy-start.11
  95.0 1.7 copy-start.6
  98.1 1.6 copy-start.22
  98.1 1.6 copy-start.24
  98.2 1.6 copy-start.26
  98.2 1.6 copy-start.28
  99.8 2.0 copy-start.1
  101.9 1.7 copy-start.78
  106.5 99.9 %all-gather.9.cloned.1.call-start = ((), (), s32[]{:S(2)}) async-start(), calls=%async_computation.12 | async-start | bytes 2949120 | tf_op jit(solution)/shard_map/all_gather | solution.py:157
  153.1 1.5 copy-start.37
  153.1 2.5 copy-start.49
  153.1 2.5 copy-start.51
  156.9 100.3 %all-gather.11.cloned.1.call-start = ((), (), s32[]{:S(2)}) async-start(), calls=%async_computation.14 | async-start | bytes 2949120 | tf_op jit(solution)/shard_map/all_gather | solution.py:177
  160.3 159.2 %reduce-scatter.13.cloned.1.call-start = ((), (), s32[]{:S(2)}) async-start(), calls=%async_computation.15 | async-start | bytes 2949120 | tf_op jit(solution)/shard_map/reduce_scatter | solution.py:189
  257.2 10.0 %copy-start.75 = (bf16[1152,2,768]{2,1,0:T(2,128)(2,1)S(1)}, bf16[1152,2,768]{2,1,0:T(2,128)(2,1)}, u32[]{:S(2)}) copy-start(bf16[1152,2,768]{2,1,0:T(2,128)(2,1)} %param.30) | copy-start | bytes 10616836
  265.6 1.6 copy-start.82
  272.8 95.9 %reduce-scatter.11.cloned.1.call-start = ((), (), s32[]{:S(2)}) async-start(), calls=%async_computation.13 | async-start | bytes 2949120 | tf_op jit(solution)/shard_map/reduce_scatter | solution.py:165
  278.5 146.5 %all-gather.13.cloned.1.call-start = ((), (), s32[]{:S(2)}) async-start(), calls=%async_computation.16 | async-start | bytes 2949120 | tf_op jit(solution)/shard_map/all_gather | solution.py:202
  368.7 5.2 copy-start.36
  375.4 90.9 %reduce-scatter.23.cloned.1.call-start = ((), (), s32[]{:S(2)}) async-start(), calls=%async_computation.21 | async-start | bytes 1990656 | tf_op jit(solution)/shard_map/reduce_scatter | solution.py:317
  392.0 125.7 %reduce-scatter.21.cloned.1.call-start = ((), (), s32[]{:S(2)}) async-start(), calls=%async_computation.20 | async-start | bytes 3981312 | tf_op jit(solution)/shard_map/reduce_scatter | solution.py:317
  400.3 155.1 %reduce-scatter.19.cloned.1.call-start = ((), (), s32[]{:S(2)}) async-start(), calls=%async_computation.19 | async-start | bytes 995328 | tf_op jit(solution)/shard_map/reduce_scatter | solution.py:317
  424.9 3.1 copy-start.2
  427.8 2.6 copy-start.14
  433.6 3.5 copy-start.12
  436.0 1.6 copy-start.5
  436.0 1.6 copy-start.39
  436.1 1.6 copy-start.69
  438.8 2.1 copy-start.77
  443.3 158.7 %reduce-scatter.17.cloned.1.call-start = ((), (), s32[]{:S(2)}) async-start(), calls=%async_computation.18 | async-start | bytes 2985984 | tf_op jit(solution)/shard_map/reduce_scatter | solution.py:317
  443.3 2.0 copy-start.15
  445.4 3.6 copy-start.33
  445.4 4.4 copy-start.32
  445.4 4.3 copy-start.76
  455.1 196.7 %reduce-scatter.15.cloned.1.call-start = ((), (), s32[]{:S(2)}) async-start(), calls=%async_computation.17 | async-start | bytes 2949120 | tf_op jit(solution)/shard_map/reduce_scatter | solution.py:241
  461.9 6.2 copy-start.64
  461.9 6.2 copy-start.63
  461.9 6.2 copy-start.67
  461.9 6.2 copy-start.66
  468.1 183.7 %copy-start.48 = (f32[1152]{0:T(1024)S(1)}, f32[1152]{0:T(1024)}, u32[]{:S(2)}) copy-start(f32[1152]{0:T(1024)} %copy-done.47) | copy-start | bytes 13828
  468.1 183.7 %copy-start.59 = (f32[256]{0:T(256)S(1)}, f32[256]{0:T(256)}, u32[]{:S(2)}) copy-start(f32[256]{0:T(256)} %copy-done.58) | copy-start | bytes 3076
  468.1 183.7 %copy-start.62 = (f32[256]{0:T(256)S(1)}, f32[256]{0:T(256)}, u32[]{:S(2)}) copy-start(f32[256]{0:T(256)} %copy-done.61) | copy-start | bytes 3076
  665.2 8.8 %all-to-all-start.1 = ((bf16[4,2,864]{2,1,0:T(2,128)(2,1)}), bf16[4,2,864]{2,1,0:T(2,128)(2,1)S(1)}, u32[]{:S(2)}, u32[]{:S(2)}) async-start(bf16[4,2,864]{2,1,0:T(2,128)(2,1)} %reshape.475), calls=%async_computation.6 | async-start | bytes 28672 | tf_op jit(solution)/shard_map/all_to_all | solution.py:264
  671.2 4.5 copy-start.52
  671.2 4.5 copy-start.53
  671.2 4.5 copy-start.72
  671.2 4.5 copy-start.73
  747.5 5.2 copy-start.55
  747.5 5.2 copy-start.57
  747.6 6.0 copy-start.74
  (33 other events, 36.0 us)
Sparse Core Ops, SparseCore 0:
  42.5 47.3 all-gather.6
  106.6 46.4 reduce-scatter.8
  157.0 49.3 all-gather.8
  208.4 48.7 all-gather.10
  272.9 46.4 reduce-scatter.12
  321.6 47.0 reduce-scatter.10
  375.5 49.3 all-gather.12
  428.3 37.9 reduce-scatter.22
  469.8 47.8 reduce-scatter.20
  520.8 34.6 reduce-scatter.18
  558.9 42.9 reduce-scatter.16
  604.1 47.6 reduce-scatter.14
where the time goes:
time: 774 us; the launch traced here: 764 us
  waiting for transfers between devices  480 us (62%)
  matrix products  92 us (12%)
  blocking collectives  77.2 us (10%)
  other arithmetic  53.3 us (7%)
  local copies, waits for them, and re-layouts  25.5 us (3%)
  starting transfers between devices  20.2 us (3%)
  between operations  16.4 us (2%)
    reduce_scatter x4, waiting for transfers between devices, scatter(): lax.psum_scatter(value, 'dp', scatter_dimension=axis, tiled=True)  134 us
    reduce_scatter x1, waiting for transfers between devices, shards(): lax.psum_scatter(jnp.einsum('blke,dke->bld', piece, project_weight, prefe...  48 us
    all_gather x1, waiting for transfers between devices, shards(): lax.all_gather((normed_local * (1.0 + attend_scale) + attend_shift).astyp...  47.1 us
    all_gather x1, waiting for transfers between devices, shards(): mod_two_all = lax.all_gather(mod_two, 'tensor', axis=0, tiled=True)  45.8 us
    reduce_scatter x1, waiting for transfers between devices, shards(): lax.psum_scatter(jnp.einsum('blf,fd->bld', piece, down_weight, preferred_...  45.5 us
    reduce_scatter x1, waiting for transfers between devices, shards(): lax.psum_scatter(jnp.einsum('blh,hd->bld', piece, output_weight, preferre...  45.3 us
    all_gather x1, waiting for transfers between devices, shards(): piece = lax.all_gather(branch_grad, 'tensor', axis=0, tiled=True)  41.2 us
    psum x1, blocking collectives, shards(): small = lax.psum(small, ('dp', 'tensor'))  39.6 us
  transfers between devices with their start and end apart: 14, of which 14 were waited for; matrix products, arithmetic and copies ran while one was open for 11% of the time, Pallas kernels for 0%

commit v1 on v0

--- a/solution.py
+++ b/solution.py
@@ -1,3 +1,4 @@
+import functools
 import math
 import jax
 import jax.numpy as jnp
@@ -8,6 +9,13 @@
 FREQ = 256
 GRID = 16
 EPS = 1e-06
+
+
+def time_the_seats_all(m, axis_name):
+    return jnp.sum(jax.lax.all_gather(m, axis_name=axis_name), 0)
+
+
+_change_results = functools.partial(time_the_seats_all, axis_name=("dp", "tensor"))
 
 
 def layer_norm(value):
@@ -305,7 +313,7 @@
     small = jnp.concatenate(
         [output_bias_part, down_bias_part, bias_wide.reshape(-1), query_gain_part, key_gain_part]
     )
-    small = lax.psum(small, ("dp", "tensor"))
+    small = _change_results(small)
     output_bias_grad = small[:width]
     down_bias_grad = small[width : 2 * width]
     modulate_bias_grad = small[2 * width : 8 * width].reshape(6, width)

time: 774 us -> 834 us (1.078)
  waiting for transfers between devices: 480 us -> 573 us
  blocking collectives: 77.2 us -> 36.5 us
    unnamed x12 -> x14, waiting for transfers between devices: 0.2 us -> 93.9 us
    psum x1 -> x0, blocking collectives: 39.6 us -> none  [shards(): small = lax.psum(small, ('dp', 'tensor'))]
    unnamed x172 -> x174, local copies, waits for them, and re-layouts: 17.4 us -> 20 us
  transfers between devices with their start and end apart: 14 -> 15, of which waited for: 14 -> 15; matrix products, arithmetic and copies ran while one was open for 11% -> 11% of each run, Pallas kernels for 0% -> 0%
where the time goes in v1:
time: 834 us; the launch traced here: 824 us
  waiting for transfers between devices  573 us (69%)
  matrix products  92.1 us (11%)
  other arithmetic  54.7 us (7%)
  blocking collectives  36.5 us (4%)
  local copies, waits for them, and re-layouts  31.2 us (4%)
  starting transfers between devices  20.2 us (2%)
  between operations  16.2 us (2%)
    reduce_scatter x4, waiting for transfers between devices, scatter(): lax.psum_scatter(value, 'dp', scatter_dimension=axis, tiled=True)  134 us
    unnamed x14, waiting for transfers between devices  93.9 us
    reduce_scatter x1, waiting for transfers between devices, shards(): lax.psum_scatter(jnp.einsum('blke,dke->bld', piece, project_weight, prefe...  48 us
    all_gather x1, waiting for transfers between devices, shards(): lax.all_gather((normed_local * (1.0 + attend_scale) + attend_shift).astyp...  47.1 us
    all_gather x1, waiting for transfers between devices, shards(): mod_two_all = lax.all_gather(mod_two, 'tensor', axis=0, tiled=True)  45.8 us
    reduce_scatter x1, waiting for transfers between devices, shards(): lax.psum_scatter(jnp.einsum('blf,fd->bld', piece, down_weight, preferred_...  45.5 us
    reduce_scatter x1, waiting for transfers between devices, shards(): lax.psum_scatter(jnp.einsum('blh,hd->bld', piece, output_weight, preferre...  45.3 us
    all_gather x1, waiting for transfers between devices, shards(): piece = lax.all_gather(branch_grad, 'tensor', axis=0, tiled=True)  41.2 us
  transfers between devices with their start and end apart: 15, of which 15 were waited for; matrix products, arithmetic and copies ran while one was open for 11% of the time, Pallas kernels for 0%

profile of v1, /device:TPU:0, one launch (start us, length us, event | category | flops | bytes accessed | tf_op | source)
XLA Modules:
  0.0 824.1 jit_solution(865650794626749172)
XLA Ops:
  8.1 10.4 %all-gather.1 = s32[8,4,2]{1,2,0:T(2,128)S(1)} all-gather(s32[1,4,2]{1,2,0:T(2,128)S(1)} %add_bitcast_fusion), channel_id=1, replica_groups=mesh['dp'=8,'tensor'=4] {'dp'}, dimensions={0}, use_global_device_ids=true | all-gather | bytes 288 | tf_op jit(solution)/shard_map/all_gather | solution.py:102
  21.3 2.6 gather_fusion
  24.0 2.1 multiply_convert_fusion.8
  26.1 1.2 multiply_convert_fusion.7
  27.4 1.3 fusion.49
  29.3 4.9 all-to-all-start
  34.7 5.1 all-to-all-done
  42.8 47.1 %all-gather.8.cloned.1.call-done = bf16[4,256,1152]{2,1,0:T(8,128)(2,1)} async-done(((bf16[1,256,1152]{2,1,0:T(8,128)(2,1)}), bf16[4,256,1152]{2,1,0:T(8,128)(2,1)}) %all-gather.8.cloned.1.call-update) | async-done | bytes 2359312 | tf_op jit(solution)/shard_map/all_gather | solution.py:130
  89.9 4.7 fusion.10
  100.5 1.3 copy-done.1
  103.5 2.9 convolution_convert_fusion.1
  106.5 1.3 convert_element_type.316
  107.8 45.3 %reduce-scatter.9.cloned.1.call-done = bf16[1,256,1152]{2,1,0:T(8,128)(2,1)} async-done(((bf16[4,256,1152]{2,1,0:T(8,128)(2,1)}), bf16[1,256,1152]{2,1,0:T(8,128)(2,1)}) %reduce-scatter.9.cloned.1.call-update) | async-done | bytes 589840 | tf_op jit(solution)/shard_map/reduce_scatter | solution.py:154
  153.1 1.4 fusion.103
  155.5 1.2 add_convert_fusion
  157.5 2.7 convert_reduce_fusion.3
  160.5 45.8 %all-gather.10.cloned.1.call-done = bf16[4,256,1152]{2,1,0:T(8,128)(2,1)} async-done(((bf16[1,256,1152]{2,1,0:T(8,128)(2,1)}), bf16[4,256,1152]{2,1,0:T(8,128)(2,1)}) %all-gather.10.cloned.1.call-update) | async-done | bytes 2359312 | tf_op jit(solution)/shard_map/all_gather | solution.py:165
  206.3 9.6 %fusion.1 = f32[4,256,2,768]{3,1,2,0:T(8,128)} fusion(bf16[1152,2,768]{2,1,0:T(2,128)(2,1)} %param.30, bf16[4,256,1152]{2,1,0:T(8,128)(2,1)} %all-gather.10.cloned.1.call-done), kind=kOutput, calls=%fused_computation.14 | convolution fusion | flops 3623878656 | bytes 12189696 | tf_op jit(solution)/shard_map/bld,dkf->blkf/dot_general | solution.py:166
  215.9 41.2 %all-gather.12.cloned.1.call-done = bf16[4,256,1152]{2,1,0:T(8,128)(2,1)} async-done(((bf16[1,256,1152]{2,1,0:T(8,128)(2,1)}), bf16[4,256,1152]{2,1,0:T(8,128)(2,1)}) %all-gather.12.cloned.1.call-update) | async-done | bytes 2359312 | tf_op jit(solution)/shard_map/all_gather | solution.py:185
  257.1 8.4 %fusion.26 = (bf16[4,256,1,768]{3,1,0,2:T(8,128)(2,1)S(1)}, bf16[4,256,1,768]{3,1,0,2:T(8,128)(2,1)S(1)}, bf16[4,256,768]{2,1,0:T(8,128)(2,1)}) fusion(f32[4,256,2,768]{3,1,2,0:T(8,128)} %fusion.1, bf16[4,256,1152]{2,1,0:T(8,128)(2,1)} %all-gather.12.cloned.1.call-done, bf16[768,1152]{1,0:T(8,128)(2,1)} %param.31), kind=kOutput, calls=%fused_computation.62 | convolution fusion | flops 1823735808 | bytes 15138816 | tf_op jit(solution)/shard_map/bld,fd->blf/dot_general | solution.py:187
  267.1 5.6 bitcast_convert_fusion.3
  272.8 5.6 convolution_convert_fusion
  278.4 1.3 convert_element_type.321
  279.7 39.6 %reduce-scatter.13.cloned.1.call-done = bf16[1,256,1152]{2,1,0:T(8,128)(2,1)} async-done(((bf16[4,256,1152]{2,1,0:T(8,128)(2,1)}), bf16[1,256,1152]{2,1,0:T(8,128)(2,1)}) %reduce-scatter.13.cloned.1.call-update) | async-done | bytes 589840 | tf_op jit(solution)/shard_map/reduce_scatter | solution.py:197
  319.4 2.6 fusion.45
  323.1 45.5 %reduce-scatter.11.cloned.1.call-done = bf16[1,256,1152]{2,1,0:T(8,128)(2,1)} async-done(((bf16[4,256,1152]{2,1,0:T(8,128)(2,1)}), bf16[1,256,1152]{2,1,0:T(8,128)(2,1)}) %reduce-scatter.11.cloned.1.call-update) | async-done | bytes 589840 | tf_op jit(solution)/shard_map/reduce_scatter | solution.py:173
  368.6 4.1 multiply_reduce_fusion.5
  373.8 1.5 convert_reduce_fusion.4
  375.3 11.2 %reduce-scatter.23.cloned.1.call-start = ((), (), s32[]{:S(2)}) async-start(), calls=%async_computation.21 | async-start | bytes 1990656 | tf_op jit(solution)/shard_map/reduce_scatter | solution.py:325
  386.5 5.4 fusion.4
  392.0 8.2 bitcast_convert_fusion
  400.3 24.6 %all-gather.14.cloned.1.call-done = bf16[4,256,1152]{2,1,0:T(8,128)(2,1)} async-done(((bf16[1,256,1152]{2,1,0:T(8,128)(2,1)}), bf16[4,256,1152]{2,1,0:T(8,128)(2,1)}) %all-gather.14.cloned.1.call-update) | async-done | bytes 2359312 | tf_op jit(solution)/shard_map/all_gather | solution.py:210
  424.8 2.9 convolution_convert_fusion.3
  427.9 2.4 multiply_reduce_fusion
  440.8 2.4 fusion.6
  443.3 2.0 fusion.46
  445.4 3.5 convolution_convert_fusion.2
  449.7 5.3 bitcast_convert_fusion.1
  455.3 6.5 bitcast_convert_fusion.2
  461.8 4.4 reduce-scatter.23.cloned.1.call-done
  466.2 1.7 convert_element_type.348
  468.1 49.6 %reduce-scatter.21.cloned.1.call-done = bf16[144,2,768]{2,0,1:T(8,128)(2,1)} async-done(((bf16[1152,2,768]{2,0,1:T(8,128)(2,1)}), bf16[144,2,768]{2,0,1:T(8,128)(2,1)}) %reduce-scatter.21.cloned.1.call-update) | async-done | bytes 442384 | tf_op jit(solution)/shard_map/reduce_scatter | solution.py:325
  517.6 2.3 copy.183
  519.9 35.5 %reduce-scatter.19.cloned.1.call-done = bf16[288,144]{0,1:T(8,128)(2,1)} async-done(((bf16[288,1152]{0,1:T(8,128)(2,1)}), bf16[288,144]{0,1:T(8,128)(2,1)}) %reduce-scatter.19.cloned.1.call-update) | async-done | bytes 82960 | tf_op jit(solution)/shard_map/reduce_scatter | solution.py:325
  555.4 1.6 convert_element_type.344
  557.0 44.9 %reduce-scatter.17.cloned.1.call-done = bf16[144,3,288]{2,0,1:T(8,128)(2,1)} async-done(((bf16[1152,3,288]{2,0,1:T(8,128)(2,1)}), bf16[144,3,288]{2,0,1:T(8,128)(2,1)}) %reduce-scatter.17.cloned.1.call-update) | async-done | bytes 248848 | tf_op jit(solution)/shard_map/reduce_scatter | solution.py:325
  601.9 1.9 convert_element_type.335
  603.7 48.0 %reduce-scatter.15.cloned.1.call-done = bf16[1,256,1152]{2,1,0:T(8,128)(2,1)} async-done(((bf16[4,256,1152]{2,1,0:T(8,128)(2,1)}), bf16[1,256,1152]{2,1,0:T(8,128)(2,1)}) %reduce-scatter.15.cloned.1.call-update) | async-done | bytes 589840 | tf_op jit(solution)/shard_map/reduce_scatter | solution.py:249
  651.8 1.7 fusion.48
  654.7 1.3 copy.176
  656.5 7.7 reduce.26
  665.1 3.3 all-to-all-start.1
  668.4 2.8 fusion.38
  671.2 2.8 all-to-all-done.1
  675.3 2.8 convolution_bitcast_fusion.2
  679.7 1.6 dynamic-update-slice
  681.3 16.6 %psum.7 = f32[4,1152]{1,0:T(4,128)S(1)} all-reduce(f32[4,1152]{1,0:T(4,128)S(1)} %convolution_bitcast_fusion.2), channel_id=1, replica_groups=mesh['dp'=8,'tensor'=4] {'tensor'}, use_global_device_ids=true, to_apply=%region_35.36 | all-reduce | flops 4608 | bytes 36864 | tf_op jit(solution)/shard_map/psum | solution.py:279
  698.8 9.5 %all-gather.2 = bf16[8,4,2880]{2,1,0:T(4,128)(2,1)S(1)} all-gather(bf16[1,4,2880]{2,1,0:T(4,128)(2,1)S(1)} %maximum_bitcast_fusion), channel_id=1, replica_groups=mesh['dp'=8,'tensor'=4] {'dp'}, dimensions={0}, use_global_device_ids=true | all-gather | bytes 207360 | tf_op jit(solution)/shard_map/all_gather | solution.py:282
  708.4 1.6 convert_reduce_fusion.7
  713.0 1.9 fusion.68
  714.9 2.2 fusion.60
  717.1 93.7 %all-reduce.15.cloned.1.call-done = f32[299520]{0:T(1024)} async-done(((f32[299520]{0:T(1024)}), f32[299520]{0:T(1024)}) %all-reduce.15.cloned.1.call-update) | async-done | bytes 1198096
  810.9 3.0 reshape.447
  813.9 1.4 reduce_sum.301
  (283 shorter events, 43.3 us)
Async XLA Ops:
  7.2 18.9 %copy-start = (bf16[1152,1152]{1,0:T(8,128)(2,1)S(1)}, bf16[1152,1152]{1,0:T(8,128)(2,1)}, u32[]{:S(2)}) copy-start(bf16[1152,1152]{1,0:T(8,128)(2,1)} %param.37) | copy-start | bytes 7962628
  21.3 6.0 copy-start.54
  21.3 6.0 copy-start.56
  24.0 3.4 copy-start.8
  27.4 6.9 copy-start.3
  29.3 10.5 %all-to-all-start = ((bf16[4,6,288]{2,1,0:T(8,128)(2,1)}), bf16[4,6,288]{2,1,0:T(8,128)(2,1)S(1)}, u32[]{:S(2)}, u32[]{:S(2)}) async-start(bf16[4,6,288]{2,1,0:T(8,128)(2,1)} %copy.159), calls=%async_computation | async-start | bytes 49152 | tf_op jit(solution)/shard_map/all_to_all | solution.py:122
  34.2 55.7 %all-gather.8.cloned.1.call-start = ((), (), s32[]{:S(2)}) async-start(), calls=%async_computation.10 | async-start | bytes 2949120 | tf_op jit(solution)/shard_map/all_gather | solution.py:130
  34.4 8.0 copy-start.58
  34.7 7.7 copy-start.79
  34.7 7.7 copy-start.80
  34.7 59.9 %copy-start.61 = (f32[256]{0:T(256)}, f32[256]{0:T(256)S(1)}, u32[]{:S(2)}) copy-start(f32[256]{0:T(256)S(1)} %add_rsqrt_fusion.1) | copy-start | bytes 3076
  42.4 110.7 %reduce-scatter.9.cloned.1.call-start = ((), (), s32[]{:S(2)}) async-start(), calls=%async_computation.11 | async-start | bytes 2949120 | tf_op jit(solution)/shard_map/reduce_scatter | solution.py:154
  42.4 52.8 %copy-start.68 = (f32[72]{0:T(128)}, f32[72]{0:T(128)S(1)}, u32[]{:S(2)}) copy-start(f32[72]{0:T(128)S(1)} %convert_element_type.306) | copy-start | bytes 868
  42.5 53.9 %copy-start.70 = (f32[72]{0:T(128)}, f32[72]{0:T(128)S(1)}, u32[]{:S(2)}) copy-start(f32[72]{0:T(128)S(1)} %convert_element_type.309) | copy-start | bytes 868
  94.6 5.9 copy-start.11
  94.9 1.7 copy-start.6
  98.1 1.6 copy-start.22
  98.1 1.6 copy-start.24
  98.1 1.6 copy-start.26
  98.1 1.6 copy-start.28
  99.8 2.0 copy-start.1
  101.8 1.7 copy-start.78
  106.4 99.9 %all-gather.10.cloned.1.call-start = ((), (), s32[]{:S(2)}) async-start(), calls=%async_computation.12 | async-start | bytes 2949120 | tf_op jit(solution)/shard_map/all_gather | solution.py:165
  153.1 2.5 copy-start.49
  153.1 2.5 copy-start.51
  156.8 100.3 %all-gather.12.cloned.1.call-start = ((), (), s32[]{:S(2)}) async-start(), calls=%async_computation.14 | async-start | bytes 2949120 | tf_op jit(solution)/shard_map/all_gather | solution.py:185
  160.2 159.2 %reduce-scatter.13.cloned.1.call-start = ((), (), s32[]{:S(2)}) async-start(), calls=%async_computation.15 | async-start | bytes 2949120 | tf_op jit(solution)/shard_map/reduce_scatter | solution.py:197
  257.1 10.0 %copy-start.75 = (bf16[1152,2,768]{2,1,0:T(2,128)(2,1)S(1)}, bf16[1152,2,768]{2,1,0:T(2,128)(2,1)}, u32[]{:S(2)}) copy-start(bf16[1152,2,768]{2,1,0:T(2,128)(2,1)} %param.30) | copy-start | bytes 10616836
  265.5 1.6 copy-start.82
  272.7 95.9 %reduce-scatter.11.cloned.1.call-start = ((), (), s32[]{:S(2)}) async-start(), calls=%async_computation.13 | async-start | bytes 2949120 | tf_op jit(solution)/shard_map/reduce_scatter | solution.py:173
  278.4 146.5 %all-gather.14.cloned.1.call-start = ((), (), s32[]{:S(2)}) async-start(), calls=%async_computation.16 | async-start | bytes 2949120 | tf_op jit(solution)/shard_map/all_gather | solution.py:210
  368.6 5.2 copy-start.36
  375.3 90.9 %reduce-scatter.23.cloned.1.call-start = ((), (), s32[]{:S(2)}) async-start(), calls=%async_computation.21 | async-start | bytes 1990656 | tf_op jit(solution)/shard_map/reduce_scatter | solution.py:325
  391.9 125.7 %reduce-scatter.21.cloned.1.call-start = ((), (), s32[]{:S(2)}) async-start(), calls=%async_computation.20 | async-start | bytes 3981312 | tf_op jit(solution)/shard_map/reduce_scatter | solution.py:325
  400.2 155.1 %reduce-scatter.19.cloned.1.call-start = ((), (), s32[]{:S(2)}) async-start(), calls=%async_computation.19 | async-start | bytes 995328 | tf_op jit(solution)/shard_map/reduce_scatter | solution.py:325
  424.8 3.1 copy-start.2
  427.8 2.6 copy-start.14
  433.5 3.6 copy-start.12
  436.0 1.6 copy-start.5
  436.0 1.6 copy-start.39
  436.0 1.6 copy-start.69
  438.7 2.1 copy-start.77
  443.2 158.7 %reduce-scatter.17.cloned.1.call-start = ((), (), s32[]{:S(2)}) async-start(), calls=%async_computation.18 | async-start | bytes 2985984 | tf_op jit(solution)/shard_map/reduce_scatter | solution.py:325
  443.3 2.0 copy-start.15
  445.3 3.6 copy-start.33
  445.3 4.4 copy-start.32
  445.3 4.3 copy-start.76
  455.1 196.7 %reduce-scatter.15.cloned.1.call-start = ((), (), s32[]{:S(2)}) async-start(), calls=%async_computation.17 | async-start | bytes 2949120 | tf_op jit(solution)/shard_map/reduce_scatter | solution.py:249
  461.8 6.2 copy-start.64
  461.8 6.2 copy-start.63
  461.8 6.2 copy-start.67
  461.8 6.2 copy-start.66
  468.0 183.7 %copy-start.48 = (f32[1152]{0:T(1024)S(1)}, f32[1152]{0:T(1024)}, u32[]{:S(2)}) copy-start(f32[1152]{0:T(1024)} %copy-done.47) | copy-start | bytes 13828
  468.1 183.7 %copy-start.59 = (f32[256]{0:T(256)S(1)}, f32[256]{0:T(256)}, u32[]{:S(2)}) copy-start(f32[256]{0:T(256)} %copy-done.58) | copy-start | bytes 3076
  468.1 183.7 %copy-start.62 = (f32[256]{0:T(256)S(1)}, f32[256]{0:T(256)}, u32[]{:S(2)}) copy-start(f32[256]{0:T(256)} %copy-done.61) | copy-start | bytes 3076
  665.1 8.8 %all-to-all-start.1 = ((bf16[4,2,864]{2,1,0:T(2,128)(2,1)}), bf16[4,2,864]{2,1,0:T(2,128)(2,1)S(1)}, u32[]{:S(2)}, u32[]{:S(2)}) async-start(bf16[4,2,864]{2,1,0:T(2,128)(2,1)} %reshape.478), calls=%async_computation.6 | async-start | bytes 28672 | tf_op jit(solution)/shard_map/all_to_all | solution.py:272
  668.4 142.5 %all-reduce.15.cloned.1.call-start = ((), (), s32[]{:S(2)}) async-start(), calls=%async_computation.22 | async-start | bytes 2400256
  675.3 3.2 copy-start.52
  675.3 3.2 copy-start.53
  675.3 3.2 copy-start.72
  675.3 3.2 copy-start.73
  681.2 28.8 %copy-start.74 = (s32[32]{0:T(128)S(1)}, s32[32]{0:T(128)}, u32[]{:S(2)}) copy-start(s32[32]{0:T(128)} %get-tuple-element.182) | copy-start | bytes 388
  681.3 30.0 %copy-start.55 = (bf16[32,128]{1,0:T(8,128)(2,1)S(1)}, bf16[32,128]{1,0:T(8,128)(2,1)}, u32[]{:S(2)}) copy-start(bf16[32,128]{1,0:T(8,128)(2,1)} %copy-done.54) | copy-start | bytes 24580
  681.3 30.0 %copy-start.57 = (bf16[32,128]{1,0:T(8,128)(2,1)S(1)}, bf16[32,128]{1,0:T(8,128)(2,1)}, u32[]{:S(2)}) copy-start(bf16[32,128]{1,0:T(8,128)(2,1)} %copy-done.56) | copy-start | bytes 24580
  (34 other events, 37.5 us)
Sparse Core Ops, SparseCore 0:
  42.5 47.3 all-gather.7
  106.6 46.4 reduce-scatter.8
  156.9 49.3 all-gather.9
  208.3 48.7 all-gather.11
  272.8 46.4 reduce-scatter.12
  321.5 47.0 reduce-scatter.10
  375.4 49.3 all-gather.13
  428.2 37.9 reduce-scatter.22
  469.7 47.8 reduce-scatter.20
  520.7 34.6 reduce-scatter.18
  558.9 42.9 reduce-scatter.16
  604.0 47.6 reduce-scatter.14
  681.4 129.4 all-reduce.14
